TPU v7x, 32 devices: a whole 2x2x4 slice. The times are simulated.
32 devices in a mesh: row: 4 (over z), col: 8 (over y, x, core).
Axes of the slice: x: 2, y: 2, z: 4, core: 2. Of those that a mesh axis runs over, the one named last changes fastest.
Arguments:
- right_side: float32 [512, 512, 512], P(('row', 'col')), may hold values from -51 to 51
- coupling: float32 [512, 512, 512], P(('row', 'col')), may hold values from 0.01 to 0.3
Outputs:
- solution: float32 [512, 512, 512], P(('row', 'col'))
- residual: float32 [512, 512, 512], P(('row', 'col'))
- residual_norm: float32 [1], replicated
All inputs are finite; a program needn't handle non-finite values.
Results may differ from a plain program's by a relative error of at most 0.0003.
Values sent between devices are 32-bit elements; how exact they have to be, the bound alone decides.
A program may use at most 192 MiB of HBM per device.

v0:
```python
import math
import jax
import jax.numpy as jnp
from jax import lax
from jax.sharding import PartitionSpec as P

HIGHEST = lax.Precision.HIGHEST


def extended(block, sides, width):
    for axis, dim in sides:
        count = lax.axis_size(axis)
        forward = [(i, i + 1) for i in range(count - 1)]
        forward.append((count - 1, 0))
        backward = [(target, source) for source, target in forward]
        low = lax.ppermute(
            lax.slice_in_dim(block, block.shape[dim] - width, None, axis=dim), axis, forward
        )
        high = lax.ppermute(lax.slice_in_dim(block, 0, width, axis=dim), axis, backward)
        block = jnp.concatenate([low, block, high], axis=dim)
    return block


def cas_table(count):
    index = jnp.arange(count, dtype=jnp.int32)
    product = index[:, None] * index[None, :] % count
    angle = product.astype(jnp.float32) * (2.0 * math.pi / count)
    return jnp.cos(angle) + jnp.sin(angle)


def wave_square(count):
    index = jnp.arange(count, dtype=jnp.int32)
    signed = jnp.where(2 * index < count, index, index - count).astype(jnp.float32)
    return jnp.square(signed * (2.0 * math.pi / count))


def along_last(field, table):
    return jnp.einsum("abx,xk->abk", field, table, precision=HIGHEST)


def along_middle(field, table):
    return jnp.einsum("ayb,yk->akb", field, table, precision=HIGHEST)


def along_first(field, table):
    return jnp.einsum("zab,zk->kab", field, table, precision=HIGHEST)


def shards(right_side, coupling):
    planes, rows, cols = right_side.shape
    depth = planes * lax.axis_size("row") * lax.axis_size("col")
    table_x = cas_table(cols)
    table_y = cas_table(rows)
    table_z = cas_table(depth)
    spectra = along_middle(along_last(right_side, table_x), table_y)
    pencil = lax.all_to_all(spectra, ("row", "col"), split_axis=1, concat_axis=0, tiled=True)
    block = lax.axis_index(("row", "col"))
    width = pencil.shape[1]
    spectrum = along_first(pencil, table_z)
    start = block * width
    wave_rows = lax.dynamic_slice_in_dim(wave_square(rows), start, width, 0)
    eigen = (
        wave_square(depth)[:, None, None]
        + wave_rows[None, :, None]
        + wave_square(cols)[None, None, :]
    )
    volume = float(depth * rows * cols)
    positive = eigen > 0
    scaled = jnp.where(positive, spectrum / jnp.where(positive, eigen * volume, 1.0), 0.0)
    lines = along_first(scaled, table_z)
    slab = lax.all_to_all(lines, ("row", "col"), split_axis=0, concat_axis=1, tiled=True)
    slab = along_middle(slab, table_y)
    solution = along_last(slab, table_x)
    padded = extended(solution, ((("row", "col"), 0),), 1)
    lap = 6.0 * solution - padded[2:] - padded[:-2]
    lap = lap - jnp.roll(solution, 1, 1) - jnp.roll(solution, -1, 1)
    lap = lap - jnp.roll(solution, 1, 2) - jnp.roll(solution, -1, 2)
    residual = right_side - (coupling * solution + lap)
    squares = lax.psum(jnp.sum(residual * residual), ("row", "col"))
    residual_norm = jnp.sqrt(squares).reshape(1)
    return (solution, residual, residual_norm)


def solution(mesh):
    in_specs = (P(("row", "col"), None, None), P(("row", "col"), None, None))
    out_specs = (P(("row", "col"), None, None), P(("row", "col"), None, None), P())
    return jax.shard_map(shards, mesh=mesh, in_specs=in_specs, out_specs=out_specs, check_vma=False)
```

profile of v0, /device:TPU:14, one launch (start us, length us, event | category | flops | bytes accessed | tf_op | source)
XLA Modules:
  0.0 1289.1 jit_solution(7548929516048661643)
XLA Ops:
  0.6 68.0 %fusion.31 = f32[512,16,512]{2,0,1:T(8,128)} fusion(f32[16,512,512]{2,1,0:T(8,128)} %param.2), kind=kOutput, calls=%fused_computation.36 | convolution fusion | flops 25773735936 | bytes 33554432 | tf_op jit(solution)/shard_map/abx,xk->abk/dot_general | solution.py:38
  68.7 79.3 %fusion.19 = f32[16,512,512]{2,1,0:T(8,128)} fusion(f32[512,16,512]{2,0,1:T(8,128)} %fusion.31), kind=kOutput, calls=%fused_computation.23 | convolution fusion | flops 25773735936 | bytes 33554432 | tf_op jit(solution)/shard_map/ayb,yk->akb/dot_general | solution.py:42
  148.0 17.8 %copy.23 = f32[16,512,512]{2,0,1:T(8,128)} copy(f32[16,512,512]{2,1,0:T(8,128)} %fusion.19) | data formatting | bytes 33554432 | tf_op jit(solution)/shard_map/ayb,yk->akb/transpose | solution.py:42
  165.8 6.0 all-to-all-start
  171.9 5.3 fusion.96
  177.2 5.3 fusion.94
  182.6 350.1 %all-to-all-done = f32[16,512,512]{2,0,1:T(8,128)} async-done(((f32[16,512,512]{2,0,1:T(8,128)}), f32[16,512,512]{2,0,1:T(8,128)}, u32[]{:S(2)}, u32[]{:S(2)}) %all-to-all-start) | async-done | bytes 16777248 | tf_op jit(solution)/shard_map/all_to_all | solution.py:56
  532.7 17.3 %copy.25 = f32[32,16,16,512]{3,2,1,0:T(8,128)S(1)} copy(f32[32,16,16,512]{3,1,2,0:T(8,128)} %bitcast.9) | data formatting | bytes 33554432 | tf_op jit(solution)/shard_map/all_to_all | solution.py:56
  550.1 79.4 %fusion.15 = f32[512,16,512]{2,0,1:T(8,128)S(1)} fusion(f32[512,16,512]{2,1,0:T(8,128)S(1)} %bitcast.54, f32[512,512,1]{1,0,2:T(8,128)} %fusion.94), kind=kOutput, calls=%fused_computation.19 | convolution fusion | flops 25769803776 | bytes 34603008 | tf_op jit(solution)/shard_map/zab,zk->kab/dot_general | solution.py:46
  629.4 40.3 %fusion.17 = f32[512,16,512]{2,0,1:T(8,128)} fusion(f32[512,16,512]{2,0,1:T(8,128)S(1)} %fusion.15, f32[512]{0:T(512)S(1)} %fusion.44, f32[512,16]{0,1:T(8,128)S(1)} %broadcast_add_fusion, f32[512,512,1]{1,0,2:T(8,128)} %fusion.96), kind=kOutput, calls=%fused_computation.22 | convolution fusion | flops 25794969600 | bytes 34637824 | tf_op jit(solution)/shard_map/zab,zk->kab/dot_general | solution.py:46
  669.8 17.9 %copy.29 = f32[512,16,512]{2,1,0:T(8,128)} copy(f32[512,16,512]{2,0,1:T(8,128)} %fusion.17) | data formatting | bytes 33554432 | tf_op jit(solution)/shard_map/zab,zk->kab/dot_general | solution.py:46
  687.7 15.5 %all-to-all-start.1 = ((f32[512,16,512]{2,1,0:T(8,128)}), f32[512,16,512]{2,1,0:T(8,128)}, u32[]{:S(2)}, u32[]{:S(2)}) async-start(f32[512,16,512]{2,1,0:T(8,128)} %copy.29), calls=%async_computation.1 | async-start | bytes 33554432 | tf_op jit(solution)/shard_map/all_to_all | solution.py:71
  703.2 4.1 fusion.92
  707.4 356.8 %all-to-all-done.1 = f32[512,16,512]{2,1,0:T(8,128)} async-done(((f32[512,16,512]{2,1,0:T(8,128)}), f32[512,16,512]{2,1,0:T(8,128)}, u32[]{:S(2)}, u32[]{:S(2)}) %all-to-all-start.1) | async-done | bytes 16777248 | tf_op jit(solution)/shard_map/all_to_all | solution.py:71
  1064.1 7.0 copy.30
  1071.2 42.4 %fusion.36 = f32[512,16,512]{2,0,1:T(8,128)} fusion(f32[16,512,512]{2,1,0:T(8,128)S(1)} %bitcast.53), kind=kOutput, calls=%fused_computation.41 | convolution fusion | flops 25773735936 | bytes 33554432 | tf_op jit(solution)/shard_map/ayb,yk->akb/dot_general | solution.py:42
  1113.6 31.4 %fusion.11 = f32[16,512,512]{2,1,0:T(8,128)S(1)} fusion(f32[512,16,512]{2,0,1:T(8,128)} %fusion.36, f32[512,512,1]{1,0,2:T(8,128)S(1)} %fusion.92), kind=kOutput, calls=%fused_computation.15 | convolution fusion | flops 25769803776 | bytes 34603008 | tf_op jit(solution)/shard_map/abx,xk->abk/dot_general | solution.py:38
  1145.0 1.6 fusion.73
  1146.6 12.9 %fusion.75 = (f32[16,511,512]{2,1,0:T(8,128)}, f32[16,511,512]{2,1,0:T(8,128)}) fusion(f32[16,512,512]{2,1,0:T(8,128)S(1)} %fusion.11), kind=kLoop, calls=%fused_computation.84 | loop fusion | bytes 66977792 | tf_op jit(solution)/shard_map/jit(_roll_static)/slice | solution.py:76
  1160.0 12.7 fusion.77
  1172.8 3.6 fusion.76
  1176.4 7.0 collective-permute-done
  1184.7 55.6 %multiply_reduce_fusion = (f32[]{:T(128)}, f32[16,512,512]{2,1,0:T(8,128)}) fusion(f32[16,512,512]{2,1,0:T(8,128)} %param.2, f32[16,512,1]{2,1,0:T(8,128)} %get-tuple-element.12, f32[16,512,511]{2,1,0:T(8,128)} %get-tuple-element.14, f32[16,512,511]{2,1,0:T(8,128)} %get-tuple-element.13, f32[16,512,1]{2,1,0:T(8,128)S(1)} %get-tuple-element.11, ...), kind=kLoop, calls=%fused_computation.21 | loop fusion | flops 75497472 | bytes 136314880 | tf_op jit(solution)/shard_map/reduce_sum | solution.py:79
  1240.3 46.4 %psum.7 = f32[]{:T(128)} all-reduce(f32[]{:T(128)} %get-tuple-element.3), channel_id=1, replica_groups=mesh['row'=4,'col'=8] {'row','col'}, use_global_device_ids=true, to_apply=%region_1.2 | all-reduce | flops 1 | bytes 8 | tf_op jit(solution)/shard_map/psum | solution.py:79
  (9 shorter events, 2.0 us)
Async XLA Ops:
  165.8 366.9 %all-to-all-start = ((f32[16,512,512]{2,0,1:T(8,128)}), f32[16,512,512]{2,0,1:T(8,128)}, u32[]{:S(2)}, u32[]{:S(2)}) async-start(f32[16,512,512]{2,0,1:T(8,128)} %copy.23), calls=%async_computation | async-start | bytes 33554432 | tf_op jit(solution)/shard_map/all_to_all | solution.py:56
  687.7 376.5 %all-to-all-start.1 = ((f32[512,16,512]{2,1,0:T(8,128)}), f32[512,16,512]{2,1,0:T(8,128)}, u32[]{:S(2)}, u32[]{:S(2)}) async-start(f32[512,16,512]{2,1,0:T(8,128)} %copy.29), calls=%async_computation.1 | async-start | bytes 33554432 | tf_op jit(solution)/shard_map/all_to_all | solution.py:71
  1145.0 27.8 %copy-start = (f32[16,512,512]{2,1,0:T(8,128)}, f32[16,512,512]{2,1,0:T(8,128)S(1)}, u32[]{:S(2)}) copy-start(f32[16,512,512]{2,1,0:T(8,128)S(1)} %fusion.11) | copy-start | bytes 50331652
  1159.5 23.9 %collective-permute-start = (f32[1,512,512]{2,1,0:T(8,128)}, f32[1,512,512]{2,1,0:T(8,128)S(1)}, u32[]{:S(2)}, u32[]{:S(2)}) collective-permute-start(f32[1,512,512]{2,1,0:T(8,128)} %get-tuple-element.5), channel_id=1, source_target_pairs={{1,0},{2,1},{3,2},{4,3},{5,4},{6,5},{7,6},{8,7},{9,8},{10,9},{11,1... | collective-permute-start | bytes 3145736 | tf_op jit(solution)/shard_map/ppermute | solution.py:19
  1159.5 25.1 %collective-permute-start.1 = (f32[1,512,512]{2,1,0:T(8,128)}, f32[1,512,512]{2,1,0:T(8,128)}, u32[]{:S(2)}, u32[]{:S(2)}) collective-permute-start(f32[1,512,512]{2,1,0:T(8,128)} %get-tuple-element.6), channel_id=1, source_target_pairs={{0,1},{1,2},{2,3},{3,4},{4,5},{5,6},{6,7},{7,8},{8,9},{9,10},{10,1... | collective-permute-start | bytes 3145736 | tf_op jit(solution)/shard_map/ppermute | solution.py:16
where the time goes:
time: 1300 us; the launch traced here: 1290 us
  waiting for transfers between devices  715 us (55%)
  matrix products  341 us (26%)
  local copies, waits for them, and re-layouts  91 us (7%)
  other arithmetic  70.5 us (5%)
  blocking collectives  46.4 us (4%)
  starting transfers between devices  22.1 us (2%)
    all_to_all x1, waiting for transfers between devices, shards(): lax.all_to_all(lines, ('row', 'col'), split_axis=0, concat_axis=1, tiled=...  357 us
    all_to_all x1, waiting for transfers between devices, shards(): lax.all_to_all(spectra, ('row', 'col'), split_axis=1, concat_axis=0, tile...  350 us
    dot_general x2, matrix products, along_middle(): return jnp.einsum('ayb,yk->akb', field, table, precision=HIGHEST)  122 us
    dot_general x2, matrix products, along_first(): return jnp.einsum('zab,zk->kab', field, table, precision=HIGHEST)  120 us
    dot_general x2, matrix products, along_last(): return jnp.einsum('abx,xk->abk', field, table, precision=HIGHEST)  99.4 us
    reduce_sum x1, other arithmetic, shards(): squares = lax.psum(jnp.sum(residual * residual), ('row', 'col'))  55.6 us
    psum x1, blocking collectives, shards(): squares = lax.psum(jnp.sum(residual * residual), ('row', 'col'))  46.4 us
  transfers between devices with their start and end apart: 4, of which 4 were waited for; matrix products, arithmetic and copies ran while one was open for 2% of the time, Pallas kernels for 0%

commit v1 on v0

--- a/solution.py
+++ b/solution.py
@@ -68,7 +68,12 @@
     positive = eigen > 0
     scaled = jnp.where(positive, spectrum / jnp.where(positive, eigen * volume, 1.0), 0.0)
     lines = along_first(scaled, table_z)
-    slab = lax.all_to_all(lines, ("row", "col"), split_axis=0, concat_axis=1, tiled=True)
+    slab = jnp.concatenate(
+        lax.all_to_all(
+            jnp.stack(jnp.split(lines, lax.axis_size(("row", "col")), axis=0)), ("row", "col"), 0, 0
+        ),
+        axis=1,
+    )
     slab = along_middle(slab, table_y)
     solution = along_last(slab, table_x)
     padded = extended(solution, ((("row", "col"), 0),), 1)

time: 1300 us -> 1240 us (0.954)
  matrix products: 341 us -> 277 us
    dot_general x2, matrix products: 120 us -> 71.6 us  [along_first(): return jnp.einsum('zab,zk->kab', field, table, precision=HIGHEST)]
    unnamed x2 -> x33, local copies, waits for them, and re-layouts: 0.01 us -> 25.7 us
    dot_general x1 -> x0, local copies, waits for them, and re-layouts: 17.9 us -> none  [along_first(): return jnp.einsum('zab,zk->kab', field, table, precision=HIGHEST)]
    dot_general x2, matrix products: 122 us -> 106 us  [along_middle(): return jnp.einsum('ayb,yk->akb', field, table, precision=HIGHEST)]
  transfers between devices with their start and end apart: 4 -> 4, of which waited for: 4 -> 4; matrix products, arithmetic and copies ran while one was open for 2% -> 3% of each run, Pallas kernels for 0% -> 0%
where the time goes in v1:
time: 1240 us; the launch traced here: 1230 us
  waiting for transfers between devices  713 us (58%)
  matrix products  277 us (22%)
  local copies, waits for them, and re-layouts  92.8 us (7%)
  other arithmetic  72.2 us (6%)
  blocking collectives  46.4 us (4%)
  starting transfers between devices  22.4 us (2%)
    all_to_all x1, waiting for transfers between devices, shards(): lax.all_to_all(spectra, ('row', 'col'), split_axis=1, concat_axis=0, tile...  352 us
    all_to_all x1, waiting for transfers between devices, shards(): lax.all_to_all(jnp.stack(jnp.split(lines, lax.axis_size(('row', 'col')),...  352 us
    dot_general x2, matrix products, along_middle(): return jnp.einsum('ayb,yk->akb', field, table, precision=HIGHEST)  106 us
    dot_general x2, matrix products, along_last(): return jnp.einsum('abx,xk->abk', field, table, precision=HIGHEST)  99.4 us
    dot_general x2, matrix products, along_first(): return jnp.einsum('zab,zk->kab', field, table, precision=HIGHEST)  71.6 us
    reduce_sum x1, other arithmetic, shards(): squares = lax.psum(jnp.sum(residual * residual), ('row', 'col'))  55.6 us
    psum x1, blocking collectives, shards(): squares = lax.psum(jnp.sum(residual * residual), ('row', 'col'))  46.4 us
    unnamed x33, local copies, waits for them, and re-layouts  25.7 us
  transfers between devices with their start and end apart: 4, of which 4 were waited for; matrix products, arithmetic and copies ran while one was open for 3% of the time, Pallas kernels for 0%

profile of v1, /device:TPU:14, one launch (start us, length us, event | category | flops | bytes accessed | tf_op | source)
XLA Modules:
  0.0 1227.2 jit_solution(7899547386904321603)
XLA Ops:
  0.6 68.0 %fusion.33 = f32[512,16,512]{2,0,1:T(8,128)} fusion(f32[16,512,512]{2,1,0:T(8,128)} %param.2), kind=kOutput, calls=%fused_computation.38 | convolution fusion | flops 25773735936 | bytes 33554432 | tf_op jit(solution)/shard_map/abx,xk->abk/dot_general | solution.py:38
  68.7 68.5 %fusion.21 = f32[16,512,512]{2,1,0:T(8,128)} fusion(f32[512,16,512]{2,0,1:T(8,128)} %fusion.33), kind=kOutput, calls=%fused_computation.25 | convolution fusion | flops 25773735936 | bytes 33554432 | tf_op jit(solution)/shard_map/ayb,yk->akb/dot_general | solution.py:42
  137.2 17.8 %copy.22 = f32[16,512,512]{2,0,1:T(8,128)} copy(f32[16,512,512]{2,1,0:T(8,128)} %fusion.21) | data formatting | bytes 33554432 | tf_op jit(solution)/shard_map/ayb,yk->akb/transpose | solution.py:42
  154.9 6.0 all-to-all-start
  161.1 4.1 fusion.133
  165.2 4.1 fusion.131
  169.4 352.5 %all-to-all-done = f32[16,512,512]{2,0,1:T(8,128)} async-done(((f32[16,512,512]{2,0,1:T(8,128)}), f32[16,512,512]{2,0,1:T(8,128)}, u32[]{:S(2)}, u32[]{:S(2)}) %all-to-all-start) | async-done | bytes 16777248 | tf_op jit(solution)/shard_map/all_to_all | solution.py:56
  521.9 17.5 %copy.24 = f32[32,16,16,512]{3,2,1,0:T(8,128)S(1)} copy(f32[32,16,16,512]{3,1,2,0:T(8,128)} %bitcast.9) | data formatting | bytes 33554432 | tf_op jit(solution)/shard_map/all_to_all | solution.py:56
  539.4 36.3 %fusion.17 = f32[512,16,512]{2,0,1:T(8,128)} fusion(f32[512,16,512]{2,1,0:T(8,128)S(1)} %bitcast.183, f32[512,512,1]{1,0,2:T(8,128)S(1)} %fusion.131), kind=kOutput, calls=%fused_computation.21 | convolution fusion | flops 25769803776 | bytes 34603008 | tf_op jit(solution)/shard_map/zab,zk->kab/dot_general | solution.py:46
  575.7 35.3 %fusion.19 = f32[512,16,512]{2,0,1:T(8,128)S(1)} fusion(f32[512,16,512]{2,0,1:T(8,128)} %fusion.17, f32[512]{0:T(512)S(1)} %fusion.77, f32[512,16]{0,1:T(8,128)S(1)} %broadcast_add_fusion, f32[512,512,1]{1,0,2:T(8,128)S(1)} %fusion.133), kind=kOutput, calls=%fused_computation.24 | convolution fusion | flops 25794969600 | bytes 34637824 | tf_op jit(solution)/shard_map/zab,zk->kab/dot_general | solution.py:46
  637.5 15.9 %all-to-all-start.1 = ((f32[32,16,16,512]{3,1,2,0:T(8,128)}), f32[32,16,16,512]{3,1,2,0:T(8,128)}, u32[]{:S(2)}, u32[]{:S(2)}) async-start(f32[32,16,16,512]{3,1,2,0:T(8,128)} %fusion.42), calls=%async_computation.1 | async-start | bytes 33554432 | tf_op jit(solution)/shard_map/all_to_all | solution.py:72
  653.5 4.1 fusion.129
  657.6 4.1 fusion.127
  661.7 352.5 %all-to-all-done.1 = f32[32,16,16,512]{3,1,2,0:T(8,128)} async-done(((f32[32,16,16,512]{3,1,2,0:T(8,128)}), f32[32,16,16,512]{3,1,2,0:T(8,128)}, u32[]{:S(2)}, u32[]{:S(2)}) %all-to-all-start.1) | async-done | bytes 16777248 | tf_op jit(solution)/shard_map/all_to_all | solution.py:72
  1014.2 37.6 %fusion.15 = f32[512,16,512]{2,0,1:T(8,128)} fusion(f32[16,512,512]{2,0,1:T(8,128)} %bitcast.44, f32[512,512,1]{1,0,2:T(8,128)S(1)} %fusion.129), kind=kOutput, calls=%fused_computation.19 | convolution fusion | flops 25769803776 | bytes 34603008 | tf_op jit(solution)/shard_map/ayb,yk->akb/dot_general | solution.py:42
  1051.7 31.4 %fusion.11 = f32[16,512,512]{2,1,0:T(8,128)S(1)} fusion(f32[512,16,512]{2,0,1:T(8,128)} %fusion.15, f32[512,512,1]{1,0,2:T(8,128)S(1)} %fusion.127), kind=kOutput, calls=%fused_computation.15 | convolution fusion | flops 25769803776 | bytes 34603008 | tf_op jit(solution)/shard_map/abx,xk->abk/dot_general | solution.py:38
  1083.2 1.6 fusion.106
  1084.8 12.9 %fusion.108 = (f32[16,511,512]{2,1,0:T(8,128)}, f32[16,511,512]{2,1,0:T(8,128)}) fusion(f32[16,512,512]{2,1,0:T(8,128)S(1)} %fusion.11), kind=kLoop, calls=%fused_computation.149 | loop fusion | bytes 66977792 | tf_op jit(solution)/shard_map/jit(_roll_static)/slice | solution.py:81
  1098.2 12.7 %fusion.110 = (f32[16,512,511]{2,1,0:T(8,128)}, f32[16,512,511]{2,1,0:T(8,128)}) fusion(f32[16,512,512]{2,1,0:T(8,128)S(1)} %fusion.11), kind=kLoop, calls=%fused_computation.151 | loop fusion | bytes 66977792 | tf_op jit(solution)/shard_map/jit(_roll_static)/slice | solution.py:82
  1111.0 3.6 fusion.109
  1114.6 7.0 collective-permute-done
  1121.6 1.3 collective-permute-done.1
  1122.9 55.6 %multiply_reduce_fusion = (f32[]{:T(128)}, f32[16,512,512]{2,1,0:T(8,128)}) fusion(f32[16,512,512]{2,1,0:T(8,128)} %param.2, f32[16,512,1]{2,1,0:T(8,128)} %get-tuple-element.12, f32[16,512,511]{2,1,0:T(8,128)} %get-tuple-element.14, f32[16,512,511]{2,1,0:T(8,128)} %get-tuple-element.13, f32[16,512,1]{2,1,0:T(8,128)S(1)} %get-tuple-element.11, ...), kind=kLoop, calls=%fused_computation.23 | loop fusion | flops 75497472 | bytes 136314880 | tf_op jit(solution)/shard_map/reduce_sum | solution.py:84
  1178.5 46.4 %psum.7 = f32[]{:T(128)} all-reduce(f32[]{:T(128)} %get-tuple-element.3), channel_id=1, replica_groups=mesh['row'=4,'col'=8] {'row','col'}, use_global_device_ids=true, to_apply=%region_1.2 | all-reduce | flops 1 | bytes 8 | tf_op jit(solution)/shard_map/psum | solution.py:84
  (40 shorter events, 27.2 us)
Async XLA Ops:
  154.9 366.9 %all-to-all-start = ((f32[16,512,512]{2,0,1:T(8,128)}), f32[16,512,512]{2,0,1:T(8,128)}, u32[]{:S(2)}, u32[]{:S(2)}) async-start(f32[16,512,512]{2,0,1:T(8,128)} %copy.22), calls=%async_computation | async-start | bytes 33554432 | tf_op jit(solution)/shard_map/all_to_all | solution.py:56
  637.5 376.6 %all-to-all-start.1 = ((f32[32,16,16,512]{3,1,2,0:T(8,128)}), f32[32,16,16,512]{3,1,2,0:T(8,128)}, u32[]{:S(2)}, u32[]{:S(2)}) async-start(f32[32,16,16,512]{3,1,2,0:T(8,128)} %fusion.42), calls=%async_computation.1 | async-start | bytes 33554432 | tf_op jit(solution)/shard_map/all_to_all | solution.py:72
  1083.2 27.8 %copy-start = (f32[16,512,512]{2,1,0:T(8,128)}, f32[16,512,512]{2,1,0:T(8,128)S(1)}, u32[]{:S(2)}) copy-start(f32[16,512,512]{2,1,0:T(8,128)S(1)} %fusion.11) | copy-start | bytes 50331652
  1097.7 23.9 %collective-permute-start = (f32[1,512,512]{2,1,0:T(8,128)}, f32[1,512,512]{2,1,0:T(8,128)S(1)}, u32[]{:S(2)}, u32[]{:S(2)}) collective-permute-start(f32[1,512,512]{2,1,0:T(8,128)} %get-tuple-element.5), channel_id=1, source_target_pairs={{1,0},{2,1},{3,2},{4,3},{5,4},{6,5},{7,6},{8,7},{9,8},{10,9},{11,1... | collective-permute-start | bytes 3145736 | tf_op jit(solution)/shard_map/ppermute | solution.py:19
  1097.7 25.1 %collective-permute-start.1 = (f32[1,512,512]{2,1,0:T(8,128)}, f32[1,512,512]{2,1,0:T(8,128)}, u32[]{:S(2)}, u32[]{:S(2)}) collective-permute-start(f32[1,512,512]{2,1,0:T(8,128)} %get-tuple-element.6), channel_id=1, source_target_pairs={{0,1},{1,2},{2,3},{3,4},{4,5},{5,6},{6,7},{7,8},{8,9},{9,10},{10,1... | collective-permute-start | bytes 3145736 | tf_op jit(solution)/shard_map/ppermute | solution.py:16
